TPU v7x, 128 devices: a whole 4x4x4 slice. The times are simulated.
128 devices in a mesh: batch: 1, t: 128 (over z, y, x, core).
Axes of the slice: x: 4, y: 4, z: 4, core: 2. Of those that a mesh axis runs over, the one named last changes fastest.
Arguments:
- z: bfloat16 [256, 16, 96, 128], P(('batch', 't'))
- w: bfloat16 [5, 3, 3, 3, 128, 128], replicated
- b: float32 [5, 128], replicated
- gamma: float32 [4, 128], replicated
- beta: float32 [4, 128], replicated
Outputs:
- output: bfloat16 [512, 32, 192, 128], P(('batch', 't'))
All inputs are finite; a program needn't handle non-finite values.
Results may differ from a plain program's by a relative error of at most 0.0145726.
Values are sent between devices in bfloat16 or wider.
A program may use at most 1 GiB of HBM per device.

v0:
```python
import jax
import jax.numpy as jnp
from jax import lax
from jax.sharding import PartitionSpec as P

GROUPS = 32
EPS = 1e-6
DN = ('NDHWC', 'DHWIO', 'NDHWC')


def solution(mesh):
    nt = mesh.shape['t']
    perm = [(i, i + 1) for i in range(nt - 1)]

    def from_prev(x, k, r):
        got = lax.ppermute(x[-k:], 't', perm)
        return jnp.where(r == 0, jnp.broadcast_to(x[:1], got.shape), got)

    def conv_full(xp, wk, bk):
        y = lax.conv_general_dilated(xp[None], wk, (1, 1, 1), ((0, 0), (1, 1), (1, 1)), dimension_numbers=DN, preferred_element_type=jnp.float32)[0]
        return (y + bk).astype(jnp.bfloat16)

    def conv(x, r, wk, bk):
        return conv_full(jnp.concatenate([from_prev(x, 2, r), x], axis=0), wk, bk)

    def gn_act(x, fw, cnt, g, be):
        n, hh, ww, c = x.shape
        xf = x.astype(jnp.float32).reshape(n, hh, ww, GROUPS, c // GROUPS)
        s1 = jnp.sum(jnp.sum(xf, axis=(1, 2, 4)) * fw[:, None], axis=0)
        s2 = jnp.sum(jnp.sum(xf * xf, axis=(1, 2, 4)) * fw[:, None], axis=0)
        s = lax.psum(jnp.stack([s1, s2]), 't')
        mean = s[0] / cnt
        inv = lax.rsqrt(s[1] / cnt - mean * mean + EPS)
        xn = ((xf - mean[:, None]) * inv[:, None]).reshape(x.shape) * g + be
        return jax.nn.silu(xn.astype(jnp.bfloat16).astype(jnp.float32)).astype(jnp.bfloat16)

    def block(x, r, fw, cnt, w, b, gamma, beta, i, j):
        h = conv(gn_act(x, fw, cnt, gamma[i], beta[i]), r, w[j], b[j])
        h = conv(gn_act(h, fw, cnt, gamma[i + 1], beta[i + 1]), r, w[j + 1], b[j + 1])
        return (x.astype(jnp.float32) + h.astype(jnp.float32)).astype(jnp.bfloat16)

    def local(z, w, b, gamma, beta):
        r = lax.axis_index('t')
        n, hh, ww, c = z.shape
        cnt1 = nt * n * hh * ww * (c // GROUPS)
        x = block(z, r, jnp.ones((n,), jnp.float32), cnt1, w, b, gamma, beta, 0, 0)
        hx = jnp.concatenate([from_prev(x, 1, r), x], axis=0)
        up = jnp.repeat(jnp.repeat(jnp.repeat(hx, 2, axis=0), 2, axis=1), 2, axis=2)
        u = conv_full(up, w[2], b[2])
        fw2 = jnp.ones((2 * n,), jnp.float32).at[0].set(jnp.where(r == 0, 0.0, 1.0))
        cnt2 = (nt * 2 * n - 1) * 4 * hh * ww * (c // GROUPS)
        return block(u, r, fw2, cnt2, w, b, gamma, beta, 2, 3)

    spec = P(('batch', 't'))
    return jax.shard_map(local, mesh=mesh, in_specs=(spec, P(), P(), P(), P()), out_specs=spec, check_vma=False)
```

profile of v0, /device:TPU:1, one launch (start us, length us, event | category | flops | bytes accessed | tf_op | source)
XLA Modules:
  0.0 732.2 jit_solution(7146892614089415887)
XLA Ops:
  0.0 1.6 convert_reduce_fusion
  2.0 68.7 %psum.28 = f32[2,32]{1,0:T(2,128)S(1)} all-reduce(f32[2,32]{1,0:T(2,128)S(1)} %pad_maximum_fusion.1), channel_id=1, replica_groups=mesh['batch'=1,'t'=128] {'t'}, use_global_device_ids=true, to_apply=%region_4.0 | all-reduce | flops 64 | bytes 512 | tf_op jit(solution)/shard_map/psum | solution.py:31
  71.1 1.4 slice_bitcast_fusion.10
  72.5 1.8 fusion.83
  74.3 2.6 collective-permute-start
  76.9 1.5 slice_bitcast_fusion.9
  78.4 7.4 %collective-permute-done = bf16[2,16,96,128]{3,1,2,0:T(8,128)(2,1)S(1)} collective-permute-done((bf16[2,16,96,128]{3,1,2,0:T(8,128)(2,1)S(1)}, bf16[2,16,96,128]{3,1,2,0:T(8,128)(2,1)S(1)}, u32[]{:S(2)}, u32[]{:S(2)}) %collective-permute-start) | collective-permute-done | bytes 786464 | tf_op jit(solution)/shard_map/ppermute | solution.py:16
  86.3 0.4 copy.25
  86.8 7.7 %fusion.77 = (f32[128]{0:T(128)S(1)}, f32[128]{0:T(128)S(1)}, f32[2,16,8,13,128]{4,2,3,1,0:T(8,128)S(1)}) fusion(pred[8,13]{0,1:T(8,128)(4,1)S(1)} %copy-done.10, f32[128]{0:T(128)S(1)} %get-tuple-element.32, bf16[5,3,3,3,128,128]{5,4,3,2,1,0:T(8,128)(2,1)} %param.8, bf16[4,16,1,7,2,128]{5,3,4,1,0,2:T(8,128)(2,1)S(1)} %slice.156, ...), kind=kOutput, calls=%fused_computation.98 | convolution fusion | flops 2831450112 | bytes 4523624 | tf_op jit(solution)/shard_map/conv_general_dilated | solution.py:20
  95.0 67.5 %psum.29 = f32[2,32]{1,0:T(2,128)S(1)} all-reduce(f32[2,32]{1,0:T(2,128)S(1)} %pad_maximum_fusion.2), channel_id=1, replica_groups=mesh['batch'=1,'t'=128] {'t'}, use_global_device_ids=true, to_apply=%region_9.10 | all-reduce | flops 64 | bytes 512 | tf_op jit(solution)/shard_map/psum | solution.py:31
  163.3 0.6 fusion.87
  163.9 2.6 collective-permute-start.1
  166.5 8.9 %collective-permute-done.1 = bf16[2,16,96,128]{3,1,2,0:T(8,128)(2,1)S(1)} collective-permute-done((bf16[2,16,96,128]{3,1,2,0:T(8,128)(2,1)S(1)}, bf16[2,16,96,128]{3,1,2,0:T(8,128)(2,1)S(1)}, u32[]{:S(2)}, u32[]{:S(2)}) %collective-permute-start.1) | collective-permute-done | bytes 786464 | tf_op jit(solution)/shard_map/ppermute | solution.py:16
  175.9 0.4 copy.28
  176.5 7.9 %fusion.98 = f32[2,16,8,13,128]{4,2,3,1,0:T(8,128)S(1)} fusion(bf16[4,16,1,7,2,128]{5,3,4,1,0,2:T(8,128)(2,1)S(1)} %slice.159, bf16[4,16,1,8,13,128]{5,3,4,1,0,2:T(8,128)(2,1)S(1)} %copy.28, bf16[5,3,3,3,128,128]{5,4,3,2,1,0:T(8,128)(2,1)} %param.8, pred[8,13]{0,1:T(8,128)(4,1)S(1)} %copy-done.10), kind=kOutput, calls=%fused_computation.127 | convolution fusion | flops 2828042240 | bytes 4522088 | tf_op jit(solution)/shard_map/conv_general_dilated | solution.py:20
  185.2 4.8 collective-permute-start.2
  190.0 4.3 collective-permute-done.2
  194.7 4.0 broadcast_in_dim.60
  198.7 7.6 %broadcast_in_dim.61 = bf16[6,32,96,2,128]{4,1,3,2,0:T(8,128)(2,1)} broadcast(bf16[6,32,96,128]{3,1,2,0:T(8,128)(2,1)} %bitcast.224), dimensions={0,1,2,4} | broadcast | bytes 14155776 | tf_op jit(solution)/shard_map/broadcast_in_dim | solution.py:48
  206.3 9.5 %pad.7 = bf16[6,32,1,200,128]{4,1,3,0,2:T(8,128)(2,1)} pad(bf16[6,32,1,192,128]{4,1,3,0,2:T(8,128)(2,1)} %bitcast.223, bf16[]{:T(256)} %constant.59), padding=0_0x0_0x0_0x1_7x0_0 | pad | bytes 19267586 | tf_op jit(solution)/shard_map/broadcast_in_dim;reshape | solution.py:20
  215.9 11.3 %copy.31 = bf16[6,32,1,8,25,128]{5,3,4,1,0,2:T(8,128)(2,1)} copy(bf16[6,32,1,8,25,128]{5,1,4,3,0,2:T(8,128)(2,1)} %bitcast.221) | data formatting | bytes 19660800 | tf_op jit(solution)/shard_map/conv_general_dilated | solution.py:20
  227.2 1.4 slice.163
  228.6 54.4 %fusion.3 = (f32[4,128]{1,0:T(4,128)S(1)}, f32[4,128]{1,0:T(4,128)S(1)}, f32[4,32,8,25,128]{4,2,3,1,0:T(8,128)}) fusion(pred[8,25]{0,1:T(8,128)(4,1)S(1)} %copy-done.9, f32[128]{0:T(128)S(1)} %get-tuple-element.30, bf16[5,3,3,3,128,128]{5,4,3,2,1,0:T(8,128)(2,1)} %param.8, bf16[6,32,1,7,2,128]{5,3,4,1,0,2:T(8,128)(2,1)S(1)} %slice.163, ...), kind=kOutput, calls=%fused_computation.14 | convolution fusion | flops 22238724096 | bytes 24515272 | tf_op jit(solution)/shard_map/conv_general_dilated | solution.py:20
  283.5 72.3 %psum.30 = f32[2,32]{1,0:T(2,128)S(1)} all-reduce(f32[2,32]{1,0:T(2,128)S(1)} %pad_maximum_fusion.3), channel_id=1, replica_groups=mesh['batch'=1,'t'=128] {'t'}, use_global_device_ids=true, to_apply=%region_16.17 | all-reduce | flops 64 | bytes 512 | tf_op jit(solution)/shard_map/psum | solution.py:31
  356.2 11.7 %copy.32 = f32[4,32,8,25,128]{4,1,3,2,0:T(8,128)} copy(f32[4,32,8,25,128]{4,2,3,1,0:T(8,128)} %get-tuple-element.43) | data formatting | bytes 26214400 | tf_op jit(solution)/shard_map/conv_general_dilated | solution.py:20
  367.9 7.4 %fusion.17 = bf16[4,32,192,128]{3,1,2,0:T(8,128)(2,1)S(1)} fusion(f32[128]{0:T(128)S(1)} %get-tuple-element.41, f32[128]{0:T(128)S(1)} %get-tuple-element.45, f32[128]{0:T(128)S(1)} %mul.205, f32[128]{0:T(128)S(1)} %sub.91, f32[128]{0:T(128)S(1)} %get-tuple-element.30, f32[4,32,1,200,128]{4,1,3,0,2:T(8,128)} %bitcast.216), kind=kLoop, calls=%fused_computation.30 | loop fusion | flops 44040192 | bytes 18876928 | tf_op jit(solution)/shard_map/convert_element_type | solution.py:35
  375.3 0.6 slice.166
  375.9 2.6 collective-permute-start.3
  378.8 33.9 %collective-permute-done.3 = bf16[2,32,192,128]{3,1,2,0:T(8,128)(2,1)S(1)} collective-permute-done((bf16[2,32,192,128]{3,1,2,0:T(8,128)(2,1)S(1)}, bf16[2,32,192,128]{3,1,2,0:T(8,128)(2,1)S(1)}, u32[]{:S(2)}, u32[]{:S(2)}) %collective-permute-start.3) | collective-permute-done | bytes 3145760 | tf_op jit(solution)/shard_map/ppermute | solution.py:16
  413.0 7.2 maximum_bitcast_fusion
  420.2 9.5 %pad.9 = bf16[6,32,1,200,128]{4,1,3,0,2:T(8,128)(2,1)} pad(bf16[6,32,1,192,128]{4,1,3,0,2:T(8,128)(2,1)} %maximum_bitcast_fusion, bf16[]{:T(256)} %constant.59), padding=0_0x0_0x0_0x1_7x0_0 | pad | bytes 19267586 | tf_op jit(solution)/shard_map/broadcast_in_dim | solution.py:20
  429.7 11.3 %copy.34 = bf16[6,32,1,8,25,128]{5,3,4,1,0,2:T(8,128)(2,1)} copy(bf16[6,32,1,8,25,128]{5,1,4,3,0,2:T(8,128)(2,1)} %bitcast.222) | data formatting | bytes 19660800 | tf_op jit(solution)/shard_map/conv_general_dilated | solution.py:20
  441.0 1.4 slice.167
  442.4 54.4 %fusion.6 = (f32[4,128]{1,0:T(4,128)S(1)}, f32[4,128]{1,0:T(4,128)S(1)}, f32[4,32,8,25,128]{4,2,3,1,0:T(8,128)}) fusion(pred[8,25]{0,1:T(8,128)(4,1)S(1)} %copy-done.9, f32[128]{0:T(128)S(1)} %copy-done.8, bf16[5,3,3,3,128,128]{5,4,3,2,1,0:T(8,128)(2,1)} %param.8, bf16[6,32,1,7,2,128]{5,3,4,1,0,2:T(8,128)(2,1)S(1)} %slice.167, ...), kind=kOutput, calls=%fused_computation.17 | convolution fusion | flops 22238724096 | bytes 24515272 | tf_op jit(solution)/shard_map/conv_general_dilated | solution.py:20
  497.2 68.1 %psum.31 = f32[2,32]{1,0:T(2,128)S(1)} all-reduce(f32[2,32]{1,0:T(2,128)S(1)} %pad_maximum_fusion.4), channel_id=1, replica_groups=mesh['batch'=1,'t'=128] {'t'}, use_global_device_ids=true, to_apply=%region_23.24 | all-reduce | flops 64 | bytes 512 | tf_op jit(solution)/shard_map/psum | solution.py:31
  565.7 11.8 %copy.35 = f32[4,32,8,25,128]{4,1,3,2,0:T(8,128)} copy(f32[4,32,8,25,128]{4,2,3,1,0:T(8,128)} %get-tuple-element.44) | data formatting | bytes 26214400 | tf_op jit(solution)/shard_map/conv_general_dilated | solution.py:20
  577.5 7.4 %fusion.21 = bf16[4,32,192,128]{3,1,2,0:T(8,128)(2,1)S(1)} fusion(f32[4,32,1,200,128]{4,1,3,0,2:T(8,128)} %bitcast.219, f32[128]{0:T(128)S(1)} %copy-done.6, f32[128]{0:T(128)S(1)} %copy-done.7, f32[128]{0:T(128)S(1)} %mul.217, f32[128]{0:T(128)S(1)} %sub.96, f32[128]{0:T(128)S(1)} %copy-done.8), kind=kLoop, calls=%fused_computation.34 | loop fusion | flops 44040192 | bytes 18876928 | tf_op jit(solution)/shard_map/convert_element_type | solution.py:35
  584.9 0.6 slice.170
  585.5 2.6 collective-permute-start.4
  588.4 33.9 %collective-permute-done.4 = bf16[2,32,192,128]{3,1,2,0:T(8,128)(2,1)S(1)} collective-permute-done((bf16[2,32,192,128]{3,1,2,0:T(8,128)(2,1)S(1)}, bf16[2,32,192,128]{3,1,2,0:T(8,128)(2,1)S(1)}, u32[]{:S(2)}, u32[]{:S(2)}) %collective-permute-start.4) | collective-permute-done | bytes 3145760 | tf_op jit(solution)/shard_map/ppermute | solution.py:16
  622.6 7.2 maximum_bitcast_fusion.1
  629.8 9.5 %pad.11 = bf16[6,32,1,200,128]{4,1,3,0,2:T(8,128)(2,1)} pad(bf16[6,32,1,192,128]{4,1,3,0,2:T(8,128)(2,1)} %maximum_bitcast_fusion.1, bf16[]{:T(256)} %constant.59), padding=0_0x0_0x0_0x1_7x0_0 | pad | bytes 19267586 | tf_op jit(solution)/shard_map/broadcast_in_dim | solution.py:20
  639.3 11.4 %copy.37 = bf16[6,32,1,8,25,128]{5,3,4,1,0,2:T(8,128)(2,1)} copy(bf16[6,32,1,8,25,128]{5,1,4,3,0,2:T(8,128)(2,1)} %bitcast.220) | data formatting | bytes 19660800 | tf_op jit(solution)/shard_map/conv_general_dilated | solution.py:20
  650.6 1.4 slice.171
  652.0 53.5 %fusion.49 = f32[4,32,8,25,128]{4,2,3,1,0:T(8,128)} fusion(bf16[6,32,1,7,2,128]{5,3,4,1,0,2:T(8,128)(2,1)S(1)} %slice.171, bf16[6,32,1,8,25,128]{5,3,4,1,0,2:T(8,128)(2,1)} %copy.37, pred[8,25]{0,1:T(8,128)(4,1)S(1)} %copy-done.9, bf16[5,3,3,3,128,128]{5,4,3,2,1,0:T(8,128)(2,1)} %param.8), kind=kOutput, calls=%fused_computation.65 | convolution fusion | flops 22212509696 | bytes 24510664 | tf_op jit(solution)/shard_map/conv_general_dilated | solution.py:20
  705.5 11.8 %copy.38 = f32[4,32,8,25,128]{4,1,3,2,0:T(8,128)} copy(f32[4,32,8,25,128]{4,2,3,1,0:T(8,128)} %fusion.49) | data formatting | bytes 26214400 | tf_op jit(solution)/shard_map/conv_general_dilated | solution.py:20
  717.3 9.5 %fusion.13 = bf16[4,32,192,128]{3,1,2,0:T(8,128)(2,1)S(1)} fusion(f32[4,32,1,200,128]{4,1,3,0,2:T(8,128)} %bitcast.218, f32[128]{0:T(128)S(1)} %copy-done.5, f32[128]{0:T(128)S(1)} %copy-done.4, f32[4,32,1,200,128]{4,1,3,0,2:T(8,128)} %bitcast.217), kind=kLoop, calls=%fused_computation.26 | loop fusion | flops 25165824 | bytes 31458304 | tf_op jit(solution)/shard_map/convert_element_type | solution.py:40
  726.9 5.1 copy.39
  (90 shorter events, 7.4 us)
Async XLA Ops:
  74.3 11.5 %collective-permute-start = (bf16[2,16,96,128]{3,1,2,0:T(8,128)(2,1)S(1)}, bf16[2,16,96,128]{3,1,2,0:T(8,128)(2,1)S(1)}, u32[]{:S(2)}, u32[]{:S(2)}) collective-permute-start(bf16[2,16,96,128]{3,1,2,0:T(8,128)(2,1)S(1)} %fusion.83), channel_id=1, source_target_pairs={{0,1},{1,2},{2,3},{3,4},{4,5},{5,6},{6,7},{7,8},{8,9},{9,10},{10,1... | collective-permute-start | bytes 2359304 | tf_op jit(solution)/shard_map/ppermute | solution.py:16
  78.3 289.6 %copy-start.3 = (f32[128]{0:T(128)}, f32[128]{0:T(128)S(1)}, u32[]{:S(2)}) copy-start(f32[128]{0:T(128)S(1)} %get-tuple-element.30) | copy-start | bytes 1540
  78.4 8.5 %copy-start.10 = (pred[8,13]{0,1:T(8,128)(4,1)S(1)}, pred[8,13]{0,1:T(8,128)(4,1)}, u32[]{:S(2)}) copy-start(pred[8,13]{0,1:T(8,128)(4,1)} %constant.86) | copy-start | bytes 316
  163.9 11.5 %collective-permute-start.1 = (bf16[2,16,96,128]{3,1,2,0:T(8,128)(2,1)S(1)}, bf16[2,16,96,128]{3,1,2,0:T(8,128)(2,1)S(1)}, u32[]{:S(2)}, u32[]{:S(2)}) collective-permute-start(bf16[2,16,96,128]{3,1,2,0:T(8,128)(2,1)S(1)} %fusion.87), channel_id=1, source_target_pairs={{0,1},{1,2},{2,3},{3,4},{4,5},{5,6},{6,7},{7,8},{8,9},{9,10},{10,1... | collective-permute-start | bytes 2359304 | tf_op jit(solution)/shard_map/ppermute | solution.py:16
  176.4 8.2 %copy-start.2 = (bf16[2,16,96,128]{3,2,1,0:T(8,128)(2,1)S(1)}, bf16[2,16,96,128]{3,2,1,0:T(8,128)(2,1)}, u32[]{:S(2)}) copy-start(bf16[2,16,96,128]{3,2,1,0:T(8,128)(2,1)} %param.7) | copy-start | bytes 2359300
  185.2 9.1 %collective-permute-start.2 = (bf16[1,16,96,128]{3,1,2,0:T(8,128)(2,1)S(1)}, bf16[1,16,96,128]{3,1,2,0:T(8,128)(2,1)S(1)}, u32[]{:S(2)}, u32[]{:S(2)}) collective-permute-start(bf16[1,16,96,128]{3,1,2,0:T(8,128)(2,1)S(1)} %slice.162), channel_id=1, source_target_pairs={{0,1},{1,2},{2,3},{3,4},{4,5},{5,6},{6,7},{7,8},{8,9},{9,10},{10,1... | collective-permute-start | bytes 1179656 | tf_op jit(solution)/shard_map/ppermute | solution.py:16
  215.9 12.7 %copy-start.9 = (pred[8,25]{0,1:T(8,128)(4,1)S(1)}, pred[8,25]{0,1:T(8,128)(4,1)}, u32[]{:S(2)}) copy-start(pred[8,25]{0,1:T(8,128)(4,1)} %constant.85) | copy-start | bytes 604
  375.3 3.2 copy-start.1
  375.9 36.8 %collective-permute-start.3 = (bf16[2,32,192,128]{3,1,2,0:T(8,128)(2,1)S(1)}, bf16[2,32,192,128]{3,1,2,0:T(8,128)(2,1)S(1)}, u32[]{:S(2)}, u32[]{:S(2)}) collective-permute-start(bf16[2,32,192,128]{3,1,2,0:T(8,128)(2,1)S(1)} %slice.166), channel_id=1, source_target_pairs={{0,1},{1,2},{2,3},{3,4},{4,5},{5,6},{6,7},{7,8},{8,9},{9,10},{10,1... | collective-permute-start | bytes 9437192 | tf_op jit(solution)/shard_map/ppermute | solution.py:16
  429.7 12.7 %copy-start.8 = (f32[128]{0:T(128)S(1)}, f32[128]{0:T(128)}, u32[]{:S(2)}) copy-start(f32[128]{0:T(128)} %get-tuple-element.33) | copy-start | bytes 1540
  565.7 11.8 %copy-start.6 = (f32[128]{0:T(128)S(1)}, f32[128]{0:T(128)}, u32[]{:S(2)}) copy-start(f32[128]{0:T(128)} %get-tuple-element.38) | copy-start | bytes 1540
  565.7 11.8 %copy-start.7 = (f32[128]{0:T(128)S(1)}, f32[128]{0:T(128)}, u32[]{:S(2)}) copy-start(f32[128]{0:T(128)} %get-tuple-element.48) | copy-start | bytes 1540
  584.9 3.2 copy-start
  585.5 36.8 %collective-permute-start.4 = (bf16[2,32,192,128]{3,1,2,0:T(8,128)(2,1)S(1)}, bf16[2,32,192,128]{3,1,2,0:T(8,128)(2,1)S(1)}, u32[]{:S(2)}, u32[]{:S(2)}) collective-permute-start(bf16[2,32,192,128]{3,1,2,0:T(8,128)(2,1)S(1)} %slice.170), channel_id=1, source_target_pairs={{0,1},{1,2},{2,3},{3,4},{4,5},{5,6},{6,7},{7,8},{8,9},{9,10},{10,1... | collective-permute-start | bytes 9437192 | tf_op jit(solution)/shard_map/ppermute | solution.py:16
  705.5 11.8 %copy-start.4 = (f32[128]{0:T(128)S(1)}, f32[128]{0:T(128)}, u32[]{:S(2)}) copy-start(f32[128]{0:T(128)} %copy-done.3) | copy-start | bytes 1540
  705.5 11.8 %copy-start.5 = (f32[128]{0:T(128)S(1)}, f32[128]{0:T(128)}, u32[]{:S(2)}) copy-start(f32[128]{0:T(128)} %get-tuple-element.29) | copy-start | bytes 1540
where the time goes:
time: 745 us; the launch traced here: 732 us
  blocking collectives  277 us (37%)
  matrix products  178 us (24%)
  local copies, waits for them, and re-layouts  128 us (17%)
  waiting for transfers between devices  88.3 us (12%)
  other arithmetic  45.4 us (6%)
  starting transfers between devices  15.2 us (2%)
    psum x4, blocking collectives, gn_act(): s = lax.psum(jnp.stack([s1, s2]), 't')  277 us
    conv_general_dilated x5, matrix products, conv_full(): lax.conv_general_dilated(xp[None], wk, (1, 1, 1), ((0, 0), (1, 1), (1, 1)...  178 us
    ppermute x5, waiting for transfers between devices, from_prev(): got = lax.ppermute(x[-k:], 't', perm)  88.3 us
    conv_general_dilated x15, local copies, waits for them, and re-layouts, conv_full(): lax.conv_general_dilated(xp[None], wk, (1, 1, 1), ((0, 0), (1, 1), (1, 1)...  75 us
    broadcast_in_dim x4, local copies, waits for them, and re-layouts, conv_full(): xp[None]  19.5 us
    convert_element_type x4, other arithmetic, gn_act(): jax.nn.silu(xn.astype(jnp.bfloat16).astype(jnp.float32))  17.2 us
    ppermute x5, starting transfers between devices, from_prev(): got = lax.ppermute(x[-k:], 't', perm)  15.2 us
  transfers between devices with their start and end apart: 5, of which 5 were waited for; matrix products, arithmetic and copies ran while one was open for 0% of the time, Pallas kernels for 0%

commit v1 on v0

v1 whole, which is shorter than its diff:
```python
import functools

import jax
import jax.numpy as jnp
import numpy as np
from jax import lax
from jax.experimental import pallas as pl
from jax.experimental.pallas import tpu as pltpu
from jax.sharding import PartitionSpec as P

F32, BF = jnp.float32, jnp.bfloat16
EPS = 1e-6
C = 128
MESH = pl.DeviceIdType.MESH
VMEM_LIMIT = 60 * 2**20


def vmem():
    return pl.BlockSpec(memory_space=pltpu.VMEM)


def dup(v):
    return jnp.concatenate([v, v], axis=1)


def all_reduce(parts, groups, cid):
    ns = len(groups)
    strides = [int(np.prod(groups[:i])) for i in range(ns)]
    np_ = len(parts)

    def kern(*refs):
        s_refs, o_ref = refs[:np_], refs[np_]
        rest = refs[np_ + 1:]
        slots, cur, ssem, rsem = rest[:ns], rest[ns], rest[ns + 1], rest[ns + 2]
        me = lax.axis_index('t')
        bar = pltpu.get_barrier_semaphore()

        def peer(i, g, st):
            d = lax.rem(lax.div(me, st), g)
            return me + (lax.rem(d + i, g) - d) * st, d

        for g, st in zip(groups, strides):
            for i in range(1, g):
                pl.semaphore_signal(bar, inc=1, device_id={'t': peer(i, g, st)[0]}, device_id_type=MESH)
        v = s_refs[0][...]
        for s in s_refs[1:]:
            v = v + s[...]
        cur[0] = v
        pl.semaphore_wait(bar, sum(g - 1 for g in groups))
        for k, (g, st) in enumerate(zip(groups, strides)):
            if k:
                cur[k] = v
            d = lax.rem(lax.div(me, st), g)
            slots[k][pl.ds(d, 1)] = v[None]
            for i in range(1, g):
                pltpu.make_async_remote_copy(cur.at[k], slots[k].at[d], ssem.at[k], rsem.at[k], device_id={'t': peer(i, g, st)[0]}, device_id_type=MESH).start()
            w = slots[k].at[pl.ds(0, g - 1)]
            pltpu.make_async_copy(w, w, rsem.at[k]).wait()
            v = jnp.sum(slots[k][...], axis=0)
        o_ref[...] = v
        for k, g in enumerate(groups):
            w = slots[k].at[pl.ds(0, g - 1)]
            pltpu.make_async_copy(w, w, ssem.at[k]).wait()

    return pl.pallas_call(
        kern, out_shape=jax.ShapeDtypeStruct((2, C), F32), in_specs=[vmem()] * np_, out_specs=vmem(),
        scratch_shapes=[pltpu.VMEM((g, 2, C), F32) for g in groups] + [pltpu.VMEM((ns, 2, C), F32), pltpu.SemaphoreType.DMA((ns,)), pltpu.SemaphoreType.DMA((ns,))],
        compiler_params=pltpu.CompilerParams(collective_id=cid, has_side_effects=True), name='sum_stats')(*parts)


def group_sum(s):
    lane = lax.broadcasted_iota(jnp.int32, s.shape, 1) % 4
    out = s
    for k in (1, 2, 3):
        up = pltpu.roll(s, C - k, 1)
        dn = pltpu.roll(s, 4 - k, 1)
        out = out + jnp.where(lane + k < 4, up, dn)
    return out


def norm_rows(s, cnt):
    s = group_sum(s)
    mean = s[0:1] / cnt
    return mean, lax.rsqrt(s[1:2] / cnt - mean * mean + EPS)


def act(x, mean, inv, g, be):
    v = (((x.astype(F32) - mean) * inv) * g + be).astype(BF).astype(F32)
    return v * jax.nn.sigmoid(v)


def shift(v, by):
    n = v.shape[0]
    row = lax.broadcasted_iota(jnp.int32, v.shape, 0)
    return jnp.where(row == (0 if by > 0 else n - 1), 0.0, pltpu.roll(v, by % n, 0))


def stats_of(h):
    hf = h.astype(F32)
    return jnp.sum(hf, axis=0, keepdims=True), jnp.sum(hf * hf, axis=0, keepdims=True)


def cost(flops):
    return pl.CostEstimate(flops=int(flops), bytes_accessed=int(8e6), transcendentals=0)


def z_stats(z):
    n, hh, ww, _ = z.shape

    def kern(z_ref, o_ref):
        o_ref[...] = jnp.zeros_like(o_ref)

        def body(i, c):
            s1, s2 = stats_of(z_ref[i // hh, i % hh])
            return c[0] + s1, c[1] + s2
        zero = jnp.zeros((1, C), F32)
        s1, s2 = lax.fori_loop(0, n * hh, body, (zero, zero))
        o_ref[0:1] = s1
        o_ref[1:2] = s2

    return pl.pallas_call(kern, out_shape=jax.ShapeDtypeStruct((2, C), F32), in_specs=[vmem()], out_specs=vmem(), cost_estimate=cost(1e7), name='z_stats')(z)


def conv_a(x, halo, s, g, be, w, b, cnt, res=None, R=8):
    n, hh, ww, _ = x.shape

    def kern(*refs):
        if res is None:
            x_ref, halo_ref, s_ref, g_ref, be_ref, w_ref, b_ref, o_ref, st_ref, A, W = refs
        else:
            x_ref, halo_ref, s_ref, g_ref, be_ref, w_ref, b_ref, res_ref, o_ref, A, W = refs
        first = lax.axis_index('t') == 0
        for q in range(4):
            for di in range(3):
                for dj in range(3):
                    t = di * 3 + dj
                    rows = pl.ds(dj * C, C)
                    W[q * 3 + di, rows, 0:C] = w_ref[q * 9 + t] if q < 3 else jnp.zeros((C, C), BF)
                    W[q * 3 + di, rows, C:2 * C] = w_ref[(q - 1) * 9 + t] if q > 0 else jnp.zeros((C, C), BF)
        mean, inv = norm_rows(s_ref[...], cnt)
        gg, bb = g_ref[...], be_ref[...]
        for q in range(4):
            A[q, 0] = jnp.zeros((ww, 3 * C), BF)
            A[q, hh + 1] = jnp.zeros((ww, 3 * C), BF)

            def arow(r, c):
                v = x_ref[q - 2, r] if q >= 2 else jnp.where(first, x_ref[0, r], halo_ref[q, r])
                v = act(v, mean, inv, gg, bb)
                A[q, r + 1, :, C:2 * C] = v.astype(BF)
                A[q, r + 1, :, 0:C] = shift(v, 1).astype(BF)
                A[q, r + 1, :, 2 * C:] = shift(v, -1).astype(BF)
                return c
            lax.fori_loop(0, hh, arow, 0, unroll=2)
        bias = dup(b_ref[...])
        t1 = t2 = jnp.zeros((1, C), F32)
        for rc in range(hh // R):
            r0 = rc * R
            parts = [A[q, pl.ds(r0 + di, R)].reshape(R * ww, 3 * C) for q in range(4) for di in range(3)]
            acc = jnp.dot(jnp.concatenate(parts, axis=1), W[...].reshape(12 * 3 * C, 2 * C), preferred_element_type=F32)
            h = (acc + bias).astype(BF)
            for f in range(2):
                hf = h[:, f * C:(f + 1) * C].reshape(R, ww, C)
                if res is None:
                    o_ref[f, pl.ds(r0, R)] = hf
                else:
                    o_ref[f, pl.ds(r0, R)] = (res_ref[f, pl.ds(r0, R)].astype(F32) + hf.astype(F32)).astype(BF)
            if res is None:
                s1, s2 = stats_of(h)
                t1 = t1 + (s1[:, :C] + s1[:, C:])
                t2 = t2 + (s2[:, :C] + s2[:, C:])
        if res is None:
            st_ref[0:1] = t1
            st_ref[1:2] = t2

    shp = jax.ShapeDtypeStruct(x.shape, BF)
    args = (x, halo, s, g, be, w, b) + (() if res is None else (res,))
    return pl.pallas_call(
        kern, in_specs=[vmem()] * len(args), out_specs=[vmem(), vmem()] if res is None else vmem(),
        out_shape=[shp, jax.ShapeDtypeStruct((2, C), F32)] if res is None else shp,
        scratch_shapes=[pltpu.VMEM((4, hh + 2, ww, 3 * C), BF), pltpu.VMEM((12, 3 * C, 2 * C), BF)],
        compiler_params=pltpu.CompilerParams(vmem_limit_bytes=VMEM_LIMIT), cost_estimate=cost(7e9), name='conv_a')(*args)


def up_conv(x, halo, w, b):
    n, hh, ww, _ = x.shape
    wp = ww + 16
    nq = n + 2

    def kern(x_ref, halo_ref, w_ref, b_ref, o_ref, st_ref, X, Wpp, Wpc, Wcp, Wcc, PP, PC, CP, CC, Q):
        first = lax.axis_index('t') == 0

        def kk(t, di, dj):
            return w_ref[t * 9 + di * 3 + dj]

        z = jnp.zeros((C, C), BF)

        def put(W, k, di, dj):
            for ti in range(2):
                W[ti, pl.ds(k * C, C), 0:C] = kk(0 if ti == 0 else 2, di, dj)
                W[ti, pl.ds(k * C, C), C:2 * C] = z if ti == 0 else kk(1, di, dj)
        for k, (di, dj) in enumerate(((0, 0), (0, 2), (2, 0), (2, 2))):
            put(Wpp, k, di, dj)
        for k, di in enumerate((0, 2)):
            put(Wpc, k, di, 1)
        for k, dj in enumerate((0, 2)):
            put(Wcp, k, 1, dj)
        put(Wcc, 0, 1, 1)

        for q in range(nq):
            X[q, 0] = jnp.zeros((wp, 2 * C), BF)
            X[q, hh + 1] = jnp.zeros((wp, 2 * C), BF)

            def xrow(r, c):
                v = x_ref[q - 2, r] if q >= 2 else jnp.where(first, x_ref[0, r], halo_ref[q, r])
                X[q, r + 1, 0:ww, C:2 * C] = v
                X[q, r + 1, ww:wp, C:2 * C] = jnp.zeros((16, C), BF)
                vf = v.astype(F32)
                X[q, r + 1, 0:ww, 0:C] = shift(vf, 1).astype(BF)
                tail = jnp.where(lax.broadcasted_iota(jnp.int32, (16, C), 0) == 0, vf[ww - 1:ww], 0.0)
                X[q, r + 1, ww:wp, 0:C] = tail.astype(BF)
                return c
            lax.fori_loop(0, hh, xrow, 0, unroll=2)

        bias = b_ref[...]
        t1 = t2 = jnp.zeros((1, C), F32)
        for q in range(nq):
            frames = (q - 1, q) if q else (q,)
            tis = (0, 1) if q else (1,)

            def taps(rows, r0, nr, cols):
                parts = [X[f, pl.ds(r0 + dr, nr), 0:(wp if cols == 0 else ww), cols:2 * C].reshape(-1, 2 * C - cols) for f in frames for dr in rows]
                return jnp.concatenate(parts, axis=1) if len(parts) > 1 else parts[0]

            def wt(W):
                k = W.shape[1]
                return W[...].reshape(2 * k, 2 * C) if q else W[1]

            half = hh // 2
            for i0, nr in ((0, half), (half, half + 1)):
                PP[pl.ds(i0, nr)] = jnp.dot(taps((0, 1), i0, nr, 0), wt(Wpp), preferred_element_type=F32).reshape(nr, wp, 2 * C)
                PC[pl.ds(i0, nr)] = jnp.dot(taps((0, 1), i0, nr, C), wt(Wpc), preferred_element_type=F32).reshape(nr, ww, 2 * C)
            for i0 in (0, half):
                CP[pl.ds(i0, half)] = jnp.dot(taps((1,), i0, half, 0), wt(Wcp), preferred_element_type=F32).reshape(half, wp, 2 * C)
                CC[pl.ds(i0, half)] = jnp.dot(taps((1,), i0, half, C), wt(Wcc), preferred_element_type=F32).reshape(half, ww, 2 * C)

            def comb(i, carry):
                a1, a2, b1, b2 = carry
                cp, cc = CP[i], CC[i]
                for pr in range(2):
                    fp = PP[i + pr] + cp
                    fc = PC[i + pr] + cc
                    for pc in range(2):
                        v = (fp[0:ww] if pc == 0 else pltpu.roll(fp, wp - 1, 0)[0:ww]) + fc
                        if q:
                            ev = (v[:, :C] + Q[pr, pc, i]) + bias
                            od = (v[:, :C] + v[:, C:]) + bias
                            ev, od = ev.astype(BF), od.astype(BF)
                            o_ref[2 * q - 2, 2 * i + pr, :, pc * C:(pc + 1) * C] = ev
                            o_ref[2 * q - 1, 2 * i + pr, :, pc * C:(pc + 1) * C] = od
                            if q >= 2:
                                e1, e2 = stats_of(ev)
                                d1, d2 = stats_of(od)
                                a1, a2, b1, b2 = a1 + e1, a2 + e2, b1 + d1, b2 + d2
                        if q < nq - 1:
                            Q[pr, pc, i] = v[:, C:]
                return a1, a2, b1, b2

            zero = jnp.zeros((1, C), F32)
            a1, a2, b1, b2 = lax.fori_loop(0, hh, comb, (zero,) * 4)
            if q == 2:
                a1 = jnp.where(first, 0.0, a1)
                a2 = jnp.where(first, 0.0, a2)
            t1 = t1 + a1 + b1
            t2 = t2 + a2 + b2
        st_ref[0:1] = t1
        st_ref[1:2] = t2

    return pl.pallas_call(
        kern, in_specs=[vmem()] * 4, out_specs=[vmem(), vmem()],
        out_shape=[jax.ShapeDtypeStruct((2 * n + 2, 2 * hh, ww, 2 * C), BF), jax.ShapeDtypeStruct((2, C), F32)],
        scratch_shapes=[pltpu.VMEM((nq, hh + 2, wp, 2 * C), BF)]
        + [pltpu.VMEM((2, k * C, 2 * C), BF) for k in (4, 2, 2, 1)]
        + [pltpu.VMEM((hh + 1, wp, 2 * C), F32), pltpu.VMEM((hh + 1, ww, 2 * C), F32), pltpu.VMEM((hh, wp, 2 * C), F32), pltpu.VMEM((hh, ww, 2 * C), F32), pltpu.VMEM((2, 2, hh, ww, C), F32)],
        compiler_params=pltpu.CompilerParams(vmem_limit_bytes=VMEM_LIMIT), cost_estimate=cost(1e10), name='up_conv')(x, halo, w, b)


def build_wb(w_ref, W):
    W[...] = jnp.zeros_like(W)
    for t in range(9):
        for d in range(3):
            k = w_ref[t * 3 + d]
            W[t, pl.ds(d * C, C), 0:C] = k
            W[t, pl.ds((d + 1) * C, C), C:2 * C] = k


def conv_b(ins, s, g, be, w, b, cnt, out_from, nf, weight0=False, fin=None, halo=False, R=8):
    _, hh, wh, _ = ins[0][0].shape
    ni = len(ins)
    ring = 3

    def kern(*refs):
        x_refs = refs[:ni]
        s_ref, g_ref, be_ref, w_ref, b_ref = refs[ni:ni + 5]
        rest = refs[ni + 5:]
        if fin is None:
            o_ref, st_ref, A, W = rest
        else:
            u_ref = rest[0]
            o_ref, A, W, T = rest[-4:]
        step = pl.program_id(0)
        first = lax.axis_index('t') == 0

        @pl.when(step == 0)
        def _():
            build_wb(w_ref, W)
            for k in range(ring):
                A[k, 0] = jnp.zeros((wh, 4 * C), BF)
                A[k, hh + 1] = jnp.zeros((wh, 4 * C), BF)
            if fin is None:
                st_ref[...] = jnp.zeros_like(st_ref)
        slot = lax.rem(step, ring)
        mean, inv = norm_rows(s_ref[...], cnt)
        mean, inv, gg, bb = dup(mean), dup(inv), dup(g_ref[...]), dup(be_ref[...])

        def fill(x_ref):
            def arow(r, c):
                v = act(x_ref[0, r], mean, inv, gg, bb)
                A[slot, r + 1, :, C:3 * C] = v.astype(BF)
                A[slot, r + 1, :, 0:C] = shift(v[:, C:], 1).astype(BF)
                A[slot, r + 1, :, 3 * C:] = shift(v[:, :C], -1).astype(BF)
                return c
            lax.fori_loop(0, hh, arow, 0, unroll=4)
        if ni == 1:
            fill(x_refs[0])
        else:
            use_halo = jnp.logical_and(step < 2, jnp.logical_not(first)) if halo else step < 2

            @pl.when(use_halo)
            def _():
                fill(x_refs[0])

            @pl.when(jnp.logical_not(use_halo))
            def _():
                fill(x_refs[1])

        @pl.when(step >= 2)
        def _():
            bias = dup(b_ref[...])
            t1 = t2 = jnp.zeros((1, C), F32)
            for rc in range(hh // R):
                r0 = rc * R
                parts = []
                for k in range(3):
                    sl = lax.rem(step + 1 + k, ring)
                    for di in range(3):
                        parts.append(A[sl, pl.ds(r0 + di, R)].reshape(R * wh, 4 * C))
                acc = jnp.dot(jnp.concatenate(parts, axis=1), W[...].reshape(36 * C, 2 * C), preferred_element_type=F32)
                h = (acc + bias).astype(BF)
                if fin is None:
                    o_ref[0, pl.ds(r0, R)] = h.reshape(R, wh, 2 * C)
                    s1, s2 = stats_of(h)
                    t1 = t1 + (s1[:, :C] + s1[:, C:])
                    t2 = t2 + (s2[:, :C] + s2[:, C:])
                else:
                    v = u_ref[0, pl.ds(r0, R)].reshape(R * wh, 2 * C).astype(F32) + h.astype(F32)
                    T[pl.ds(0, R * wh, stride=2), :] = v[:, :C]
                    T[pl.ds(1, R * wh, stride=2), :] = v[:, C:]
                    o_ref[0, pl.ds(r0, R)] = T[...].astype(BF).reshape(R, 2 * wh, C)
            if fin is None:
                if weight0:
                    drop = jnp.logical_and(first, step == 2)
                    t1 = jnp.where(drop, 0.0, t1)
                    t2 = jnp.where(drop, 0.0, t2)
                st_ref[0:1] += t1
                st_ref[1:2] += t2

    def full(shape):
        return pl.BlockSpec(shape, lambda i: (0,) * len(shape))
    fb = (1, hh, wh, 2 * C)
    specs = [pl.BlockSpec(fb, functools.partial(lambda m, i: (m(i), 0, 0, 0), m)) for _, m in ins]
    specs += [full((2, C)), full((1, C)), full((1, C)), full((27, C, C)), full((1, C))]
    args = [a for a, _ in ins] + [s, g, be, w, b]
    scratch = [pltpu.VMEM((ring, hh + 2, wh, 4 * C), BF), pltpu.VMEM((9, 4 * C, 2 * C), BF)]
    alias = {}
    if fin is None:
        out_shape = [jax.ShapeDtypeStruct((nf, hh, wh, 2 * C), BF), jax.ShapeDtypeStruct((2, C), F32)]
        out_specs = [pl.BlockSpec(fb, lambda i: (jnp.maximum(i - 2, 0), 0, 0, 0)), full((2, C))]
    else:
        u, u0, y = fin
        specs.append(pl.BlockSpec(fb, lambda i: (jnp.maximum(i - 2, 0) + u0, 0, 0, 0)))
        args.append(u)
        if y is not None:
            specs.append(pl.BlockSpec(memory_space=pl.ANY))
            alias = {len(args): 0}
            args.append(y)
        scratch.append(pltpu.VMEM((2 * R * wh, C), F32))
        out_shape = jax.ShapeDtypeStruct((4, hh, 2 * wh, C), BF)
        out_specs = pl.BlockSpec((1, hh, 2 * wh, C), lambda i: (jnp.maximum(i - 2, 0) + out_from, 0, 0, 0))
    return pl.pallas_call(
        kern, grid=(nf + 2,), in_specs=specs, out_specs=out_specs, out_shape=out_shape, scratch_shapes=scratch, input_output_aliases=alias,
        compiler_params=pltpu.CompilerParams(dimension_semantics=('arbitrary',), vmem_limit_bytes=VMEM_LIMIT), cost_estimate=cost(nf * 7e9), name='conv_b')(*args)


def solution(mesh):
    nt = mesh.shape['t']
    perm = [(i, i + 1) for i in range(nt - 1)]
    groups = (8, nt // 8)

    def shift_t(x):
        return lax.ppermute(x, 't', perm)

    def local(z, w, b, gamma, beta):
        n, hh, ww, c = z.shape
        wf = [w[i].reshape(27, C, C) for i in range(5)]
        row = lambda a, i: a[i:i + 1]
        cnt1 = float(nt * n * hh * ww * 4)
        cnt2 = float((nt * 2 * n - 1) * 4 * hh * ww * 4)
        zh = shift_t(z)
        s0 = all_reduce([z_stats(z)], groups, 0)
        h, p = conv_a(z, zh, s0, row(gamma, 0), row(beta, 0), wf[0], row(b, 0), cnt1)
        hh_ = shift_t(h)
        s1 = all_reduce([p], groups, 1)
        x = conv_a(h, hh_, s1, row(gamma, 1), row(beta, 1), wf[1], row(b, 1), cnt1, res=z)
        u, p = up_conv(x, shift_t(x), wf[2], row(b, 2))
        s2 = all_reduce([p], groups, 2)
        a3 = (s2, row(gamma, 2), row(beta, 2), wf[3], row(b, 3), cnt2)
        hi, p1 = conv_b([(u, lambda i: i + 2)], *a3, 0, 2)
        hal = shift_t(hi)
        lo, p0 = conv_b([(u, lambda i: i)], *a3, 0, 2, weight0=True)
        s3 = all_reduce([p0, p1], groups, 3)
        a4 = (s3, row(gamma, 3), row(beta, 3), wf[4], row(b, 4), cnt2)
        before = lambda i: jnp.minimum(i, 1)
        after = lambda i: jnp.maximum(i - 2, 0)
        y = conv_b([(lo, before), (hi, after)], *a4, 2, 2, fin=(u, 4, None))
        y = conv_b([(hal, before), (lo, after)], *a4, 0, 2, fin=(u, 2, y), halo=True)
        return y

    spec = P(('batch', 't'))
    return jax.shard_map(local, mesh=mesh, in_specs=(spec, P(), P(), P(), P()), out_specs=spec, check_vma=False)
```

time: 745 us -> 248 us (0.33); the launches traced: 732 us -> 247 us
  blocking collectives: 277 us -> 0 us
  Pallas kernels: 0 us -> 213 us
  matrix products: 178 us -> 0 us
  local copies, waits for them, and re-layouts: 128 us -> 11.7 us
  waiting for transfers between devices: 88.3 us -> 8.72 us
  other arithmetic: 45.4 us -> 0 us
    psum x4 -> x0, blocking collectives: 277 us -> none  [gn_act(): s = lax.psum(jnp.stack([s1, s2]), 't')]
    pallas_call x0 -> x12, Pallas kernels: none -> 213 us  [the longest x4 101 us: conv_b(): pl.pallas_call(kern, grid=(nf + 2,), in_specs=specs, out_specs=out_specs,...]
    conv_general_dilated x5 -> x0, matrix products: 178 us -> none  [conv_full(): lax.conv_general_dilated(xp[None], wk, (1, 1, 1), ((0, 0), (1, 1), (1, 1)...]
    ppermute x5 -> x4, waiting for transfers between devices: 88.3 us -> 8.72 us  [shift_t(): return lax.ppermute(x, 't', perm)]
    conv_general_dilated x15 -> x0, local copies, waits for them, and re-layouts: 75 us -> none  [conv_full(): lax.conv_general_dilated(xp[None], wk, (1, 1, 1), ((0, 0), (1, 1), (1, 1)...]
    broadcast_in_dim x11 -> x0, local copies, waits for them, and re-layouts: 32 us -> none  [the longest x4 19.5 us: conv_full(): xp[None]]
    convert_element_type x6 -> x0, other arithmetic: 27.1 us -> none  [the longest x4 17.2 us: gn_act(): jax.nn.silu(xn.astype(jnp.bfloat16).astype(jnp.float32))]
    broadcast_in_dim x4 -> x0, other arithmetic: 14.7 us -> none  [conv_full(): xp[None]]
  transfers between devices with their start and end apart: 5 -> 4, of which waited for: 5 -> 1; matrix products, arithmetic and copies ran while one was open for 0% -> 3% of each run, Pallas kernels for 0% -> 43%
where the time goes in v1:
time: 248 us; the launch traced here: 247 us
  Pallas kernels  213 us (86%)
  starting transfers between devices  13.4 us (5%)
  local copies, waits for them, and re-layouts  11.7 us (5%)
  waiting for transfers between devices  8.72 us (4%)
    pallas_call x4, Pallas kernels, conv_b(): pl.pallas_call(kern, grid=(nf + 2,), in_specs=specs, out_specs=out_specs,...  101 us
    pallas_call x4, Pallas kernels, all_reduce(): pl.pallas_call(kern, out_shape=jax.ShapeDtypeStruct((2, C), F32), in_spec...  70.1 us
    pallas_call x1, Pallas kernels, up_conv(): pl.pallas_call(kern, in_specs=[vmem()] * 4, out_specs=[vmem(), vmem()], o...  21.9 us
    pallas_call x2, Pallas kernels, conv_a(): pl.pallas_call(kern, in_specs=[vmem()] * len(args), out_specs=[vmem(), vm...  17.7 us
    ppermute x4, starting transfers between devices, shift_t(): return lax.ppermute(x, 't', perm)  13.4 us
    ppermute x4, waiting for transfers between devices, shift_t(): return lax.ppermute(x, 't', perm)  8.72 us
  transfers between devices with their start and end apart: 4, of which 1 were waited for; matrix products, arithmetic and copies ran while one was open for 3% of the time, Pallas kernels for 43%

profile of v1, /device:TPU:1, one launch (start us, length us, event | category | flops | bytes accessed | tf_op | source)
XLA Modules:
  0.0 247.1 jit_solution(18414545098101558181)
XLA Ops:
  0.0 4.5 %collective-permute-start = (bf16[2,16,96,128]{3,2,1,0:T(8,128)(2,1)}, bf16[2,16,96,128]{3,2,1,0:T(8,128)(2,1)S(1)}, u32[]{:S(2)}, u32[]{:S(2)}) collective-permute-start(bf16[2,16,96,128]{3,2,1,0:T(8,128)(2,1)} %refs_7_.1), channel_id=1, source_target_pairs={{0,1},{1,2},{2,3},{3,4},{4,5},{5,6},{6,7},{7,8},{8,9},{9,10},{10,1... | collective-permute-start | bytes 2359304 | tf_op jit(solution)/shard_map/ppermute | solution.py:410
  4.5 2.5 z_stats.1.refs_0_
  7.0 18.0 %sum_stats.4.refs_2_ = f32[2,128]{1,0:T(2,128)} custom-call(f32[2,128]{1,0:T(2,128)} %z_stats.1.refs_0_), custom_call_target="tpu_custom_call" | custom-call | tf_op jit(solution)/shard_map/sum_stats/pallas_call | solution.py:65
  25.0 1.4 fusion.3
  26.5 1.5 fusion.1
  28.0 4.4 %fusion = (bf16[1,3,3,3,128,128]{5,4,3,2,1,0:T(8,128)(2,1)}, bf16[1,3,3,3,128,128]{5,4,3,2,1,0:T(8,128)(2,1)}, bf16[1,3,3,3,128,128]{5,4,3,2,1,0:T(8,128)(2,1)},...) fusion(bf16[5,3,3,3,128,128]{5,4,3,2,1,0:T(8,128)(2,1)} %param.6), kind=kLoop, calls=%fused_computation | loop fusion | bytes 8847360 | tf_op jit(solution)/shard_map/slice | solution.py:414
  32.4 0.0 collective-permute-done.refs_1_
  32.4 0.0 copy-start.1
  32.4 0.9 copy-done.1
  33.3 8.7 %conv_a.2 = (bf16[2,16,96,128]{3,2,1,0:T(8,128)(2,1)}, f32[2,128]{1,0:T(2,128)}) custom-call(bf16[2,16,96,128]{3,2,1,0:T(8,128)(2,1)} %refs_7_.1, bf16[2,16,96,128]{3,2,1,0:T(8,128)(2,1)} %copy-done.1, f32[2,128]{1,0:T(2,128)} %sum_stats.4.refs_2_, f32[1,128]{1,0:T(1,128)} %get-tuple-element.37.refs_3_, f32[1,128]{1,0:T(1,128)} %get-tuple-element.40.refs_4_, ...), custom_call_target="tpu_custom_call" | custom-call | flops 7000000000 | bytes 8000000 | tf_op jit(solution)/shard_map/conv_a/pallas_call | solution.py:177
  42.0 1.9 collective-permute-start.1
  43.9 18.5 %sum_stats.5.refs_2_ = f32[2,128]{1,0:T(2,128)} custom-call(f32[2,128]{1,0:T(2,128)} %get-tuple-element.14.refs_0_), custom_call_target="tpu_custom_call" | custom-call | tf_op jit(solution)/shard_map/sum_stats/pallas_call | solution.py:65
  62.4 0.0 collective-permute-done.1.refs_1_
  62.4 0.0 copy-start.2
  62.4 0.9 copy-done.2
  63.3 9.0 %conv_a.3.x_ref = bf16[2,16,96,128]{3,2,1,0:T(8,128)(2,1)} custom-call(bf16[2,16,96,128]{3,2,1,0:T(8,128)(2,1)} %get-tuple-element.13.refs_0_, bf16[2,16,96,128]{3,2,1,0:T(8,128)(2,1)} %copy-done.2, f32[2,128]{1,0:T(2,128)} %sum_stats.5.refs_2_, f32[1,128]{1,0:T(1,128)} %get-tuple-element.36.refs_3_, f32[1,128]{1,0:T(1,128)} %get-tuple-element.41.refs_4_, ...), custom_call_target="tpu_custom_call" | custom-call | flops 7000000000 | bytes 8000000 | tf_op jit(solution)/shard_map/conv_a/pallas_call | solution.py:177
  72.3 2.1 collective-permute-start.2
  74.4 8.7 %collective-permute-done.2.halo_ref = bf16[2,16,96,128]{3,2,1,0:T(8,128)(2,1)S(1)} collective-permute-done((bf16[2,16,96,128]{3,2,1,0:T(8,128)(2,1)}, bf16[2,16,96,128]{3,2,1,0:T(8,128)(2,1)S(1)}, u32[]{:S(2)}, u32[]{:S(2)}) %collective-permute-start.2) | collective-permute-done | bytes 786464 | tf_op jit(solution)/shard_map/ppermute | solution.py:410
  83.1 0.0 copy-start.3
  83.1 0.9 copy-done.3
  84.0 21.9 %up_conv.1 = (bf16[6,32,96,256]{3,2,1,0:T(8,128)(2,1)}, f32[2,128]{1,0:T(2,128)}) custom-call(bf16[2,16,96,128]{3,2,1,0:T(8,128)(2,1)} %conv_a.3.x_ref, bf16[2,16,96,128]{3,2,1,0:T(8,128)(2,1)} %copy-done.3, bf16[27,128,128]{2,1,0:T(8,128)(2,1)} %bitcast.9, f32[1,128]{1,0:T(1,128)} %get-tuple-element.27.b_ref), custom_call_target="tpu_custom_call" | custom-call | flops 10000000000 | bytes 8000000 | tf_op jit(solution)/shard_map/up_conv/pallas_call | solution.py:278
  105.9 16.8 %sum_stats.6.refs_1_ = f32[2,128]{1,0:T(2,128)} custom-call(f32[2,128]{1,0:T(2,128)} %get-tuple-element.16.refs_0_), custom_call_target="tpu_custom_call" | custom-call | tf_op jit(solution)/shard_map/sum_stats/pallas_call | solution.py:65
  122.7 24.8 %conv_b.4 = (bf16[2,32,96,256]{3,2,1,0:T(8,128)(2,1)}, f32[2,128]{1,0:T(2,128)}) custom-call(bf16[6,32,96,256]{3,2,1,0:T(8,128)(2,1)} %get-tuple-element.15.refs_0_.refs_7_, f32[2,128]{1,0:T(2,128)} %sum_stats.6.refs_1_, f32[1,128]{1,0:T(1,128)} %get-tuple-element.38.refs_2_, f32[1,128]{1,0:T(1,128)} %get-tuple-element.39.refs_3_, ...), custom_call_target="tpu_custom_call" | custom-call | flops 14000000000 | bytes 8000000 | tf_op jit(solution)/shard_map/conv_b/pallas_call | solution.py:399
  147.5 4.9 %collective-permute-start.3 = (bf16[2,32,96,256]{3,2,1,0:T(8,128)(2,1)}, bf16[2,32,96,256]{3,2,1,0:T(8,128)(2,1)S(1)}, u32[]{:S(2)}, u32[]{:S(2)}) collective-permute-start(bf16[2,32,96,256]{3,2,1,0:T(8,128)(2,1)} %get-tuple-element.17.refs_1_), channel_id=1, source_target_pairs={{0,1},{1,2},{2,3},{3,4},{4,5},{5,6},{6,7},{7,8},{8,9},{9,10},{10,1... | collective-permute-start | bytes 9437192 | tf_op jit(solution)/shard_map/ppermute | solution.py:410
  152.4 24.9 %conv_b.5 = (bf16[2,32,96,256]{3,2,1,0:T(8,128)(2,1)}, f32[2,128]{1,0:T(2,128)}) custom-call(bf16[6,32,96,256]{3,2,1,0:T(8,128)(2,1)} %get-tuple-element.15.refs_0_.refs_7_, f32[2,128]{1,0:T(2,128)} %sum_stats.6.refs_1_, f32[1,128]{1,0:T(1,128)} %get-tuple-element.38.refs_2_, f32[1,128]{1,0:T(1,128)} %get-tuple-element.39.refs_3_, ...), custom_call_target="tpu_custom_call" | custom-call | flops 14000000000 | bytes 8000000 | tf_op jit(solution)/shard_map/conv_b/pallas_call | solution.py:399
  177.3 16.8 %sum_stats.7.refs_2_ = f32[2,128]{1,0:T(2,128)} custom-call(f32[2,128]{1,0:T(2,128)} %get-tuple-element.19.refs_0_, f32[2,128]{1,0:T(2,128)} %get-tuple-element.20.refs_1_), custom_call_target="tpu_custom_call" | custom-call | tf_op jit(solution)/shard_map/sum_stats/pallas_call | solution.py:65
  194.0 25.7 %conv_b.6.refs_8_ = bf16[4,32,192,128]{3,2,1,0:T(8,128)(2,1)} custom-call(bf16[2,32,96,256]{3,2,1,0:T(8,128)(2,1)} %get-tuple-element.18.refs_0_.refs_1_, bf16[2,32,96,256]{3,2,1,0:T(8,128)(2,1)} %get-tuple-element.17.refs_1_, f32[2,128]{1,0:T(2,128)} %sum_stats.7.refs_2_, f32[1,128]{1,0:T(1,128)} %get-tuple-element.35.refs_3_, ...), custom_call_target="tpu_custom_call" | custom-call | flops 14000000000 | bytes 8000000 | tf_op jit(solution)/shard_map/conv_b/pallas_call | solution.py:399
  219.7 0.0 collective-permute-done.3.refs_0_
  219.8 0.0 copy-start
  219.8 1.6 copy-done
  221.4 25.7 %conv_b.7 = bf16[4,32,192,128]{3,2,1,0:T(8,128)(2,1)} custom-call(bf16[2,32,96,256]{3,2,1,0:T(8,128)(2,1)} %copy-done, bf16[2,32,96,256]{3,2,1,0:T(8,128)(2,1)} %get-tuple-element.18.refs_0_.refs_1_, f32[2,128]{1,0:T(2,128)} %sum_stats.7.refs_2_, f32[1,128]{1,0:T(1,128)} %get-tuple-element.35.refs_3_, ...), custom_call_target="tpu_custom_call", output_to_operand_aliasing={{}: (8, {})} | custom-call | flops 14000000000 | bytes 8000000 | tf_op jit(solution)/shard_map/conv_b/pallas_call | solution.py:399
Async XLA Ops:
  0.0 32.4 %collective-permute-start = (bf16[2,16,96,128]{3,2,1,0:T(8,128)(2,1)}, bf16[2,16,96,128]{3,2,1,0:T(8,128)(2,1)S(1)}, u32[]{:S(2)}, u32[]{:S(2)}) collective-permute-start(bf16[2,16,96,128]{3,2,1,0:T(8,128)(2,1)} %refs_7_.1), channel_id=1, source_target_pairs={{0,1},{1,2},{2,3},{3,4},{4,5},{5,6},{6,7},{7,8},{8,9},{9,10},{10,1... | collective-permute-start | bytes 2359304 | tf_op jit(solution)/shard_map/ppermute | solution.py:410
  32.4 0.9 copy-start.1
  42.0 20.4 %collective-permute-start.1 = (bf16[2,16,96,128]{3,2,1,0:T(8,128)(2,1)}, bf16[2,16,96,128]{3,2,1,0:T(8,128)(2,1)S(1)}, u32[]{:S(2)}, u32[]{:S(2)}) collective-permute-start(bf16[2,16,96,128]{3,2,1,0:T(8,128)(2,1)} %get-tuple-element.13.refs_0_), channel_id=1, source_target_pairs={{0,1},{1,2},{2,3},{3,4},{4,5},{5,6},{6,7},{7,8},{8,9},{9,10},{10,1... | collective-permute-start | bytes 2359304 | tf_op jit(solution)/shard_map/ppermute | solution.py:410
  62.4 0.9 copy-start.2
  72.3 10.8 %collective-permute-start.2 = (bf16[2,16,96,128]{3,2,1,0:T(8,128)(2,1)}, bf16[2,16,96,128]{3,2,1,0:T(8,128)(2,1)S(1)}, u32[]{:S(2)}, u32[]{:S(2)}) collective-permute-start(bf16[2,16,96,128]{3,2,1,0:T(8,128)(2,1)} %conv_a.3.x_ref), channel_id=1, source_target_pairs={{0,1},{1,2},{2,3},{3,4},{4,5},{5,6},{6,7},{7,8},{8,9},{9,10},{10,1... | collective-permute-start | bytes 2359304 | tf_op jit(solution)/shard_map/ppermute | solution.py:410
  83.1 0.9 copy-start.3
  147.5 72.3 %collective-permute-start.3 = (bf16[2,32,96,256]{3,2,1,0:T(8,128)(2,1)}, bf16[2,32,96,256]{3,2,1,0:T(8,128)(2,1)S(1)}, u32[]{:S(2)}, u32[]{:S(2)}) collective-permute-start(bf16[2,32,96,256]{3,2,1,0:T(8,128)(2,1)} %get-tuple-element.17.refs_1_), channel_id=1, source_target_pairs={{0,1},{1,2},{2,3},{3,4},{4,5},{5,6},{6,7},{7,8},{8,9},{9,10},{10,1... | collective-permute-start | bytes 9437192 | tf_op jit(solution)/shard_map/ppermute | solution.py:410
  219.8 1.6 copy-start
